TPU v7x, 32 devices: a whole 2x2x4 slice. The times are simulated.
32 devices in a mesh: gy: 8 (over y, x, core), gx: 4 (over z).
Axes of the slice: x: 2, y: 2, z: 4, core: 2. Of those that a mesh axis runs over, the one named last changes fastest.
Arguments:
- tracer: float32 [8, 1024, 1024], P(None, 'gy', 'gx'), may hold values from -6 to 6
- east_speed: float32 [8, 1024, 1024], P(None, 'gy', 'gx'), may hold values from -0.25 to 0.25
- north_speed: float32 [8, 1024, 1024], P(None, 'gy', 'gx'), may hold values from -0.25 to 0.25
- columns: int32 [1024, 1024], P('gy', 'gx'), may hold values from 0 to 8
- thickness: float32 [8], replicated, may hold values from 0.5 to 2
- surface_flux: float32 [1024, 1024], P('gy', 'gx'), may hold values from -6 to 6
- helm: float32 [1024, 1024], P('gy', 'gx'), may hold values from 0.2 to 4
Outputs:
- tracer_new: float32 [8, 1024, 1024], P(None, 'gy', 'gx')
- heights: float32 [1024, 1024], P('gy', 'gx')
Inputs may be any that keep to these rules, and one draw needn't show every extreme that they name: `columns`: ocean levels per column; 0 means land.
All inputs are finite; a program needn't handle non-finite values.
Results may differ from a plain program's by a relative error of at most 0.0001.
Values sent between devices are 32-bit elements; how exact they have to be, the bound alone decides.
A program may use at most 64 MiB of HBM per device.

v0:
```python
import jax
import jax.numpy as jnp
from jax import lax
from jax.sharding import PartitionSpec as P

TSTEPS = 2
ITERS = 3


def extended_2(array, sides, width, wrap):
    for axis, dim in sides:
        peers, length = (lax.axis_size(axis), array.shape[dim])
        up = [(i, (i + 1) % peers) for i in range(peers if wrap else peers - 1)]
        down = [(j, i) for i, j in up]
        last = lax.slice_in_dim(array, length - width, length, axis=dim)
        first = lax.slice_in_dim(array, 0, width, axis=dim)
        before = lax.ppermute(last, axis, up)
        after = lax.ppermute(first, axis, down)
        array = jnp.concatenate([before, array, after], axis=dim)
    return array


def upwind(speed, behind, ahead):
    return jnp.maximum(speed, 0.0) * behind + jnp.minimum(speed, 0.0) * ahead


def advect_block(extended, east_ext, north_ext, ocean_ext):
    centre = extended[:, 1:-1, 1:-1]
    open_east = ocean_ext[:, 1:-1, :-1] * ocean_ext[:, 1:-1, 1:]
    flux_east = open_east * upwind(
        east_ext[:, 1:-1, :-1], extended[:, 1:-1, :-1], extended[:, 1:-1, 1:]
    )
    open_north = ocean_ext[:, :-1, 1:-1] * ocean_ext[:, 1:, 1:-1]
    flux_north = open_north * upwind(
        north_ext[:, :-1, 1:-1], extended[:, :-1, 1:-1], extended[:, 1:, 1:-1]
    )
    return centre - (
        flux_east[:, :, 1:] - flux_east[:, :, :-1] + flux_north[:, 1:, :] - flux_north[:, :-1, :]
    )


def stencil(extended, wet_ext, diagonal_term):
    weighted = wet_ext * extended
    edges = weighted[1:-1, 2:] + weighted[1:-1, :-2] + weighted[2:, 1:-1] + weighted[:-2, 1:-1]
    corners = weighted[2:, 2:] + weighted[2:, :-2] + weighted[:-2, 2:] + weighted[:-2, :-2]
    return diagonal_term * extended[1:-1, 1:-1] - wet_ext[1:-1, 1:-1] * (edges + 0.5 * corners)


def wrap_columns(source):
    return jnp.concatenate([source[:, -1:], source, source[:, :1]], axis=1)


def solve(forcing, diagonal_term, apply_matrix, sum_all):
    heights = jnp.zeros_like(forcing)
    residual = forcing
    scaled = residual / diagonal_term
    applied = apply_matrix(scaled)
    product_now, curvature = sum_all((jnp.sum(residual * scaled), jnp.sum(applied * scaled)))
    step_size = product_now / curvature
    direction = scaled
    along = applied
    for iteration in range(ITERS):
        heights = heights + step_size * direction
        residual = residual - step_size * along
        if iteration + 1 < ITERS:
            scaled = residual / diagonal_term
            applied = apply_matrix(scaled)
            product_next, curvature = sum_all(
                (jnp.sum(residual * scaled), jnp.sum(applied * scaled))
            )
            factor = product_next / product_now
            step_size = product_next / (curvature - factor * product_next / step_size)
            direction = scaled + factor * direction
            along = applied + factor * along
            product_now = product_next
    return heights


def on_device(tracer, east_speed, north_speed, columns, thickness, surface_flux, helm):
    levels, rows_dev, cols_dev = tracer.shape
    depth = lax.broadcasted_iota(jnp.int32, tracer.shape, 0)
    ocean = (depth < columns[None]).astype(jnp.float32)
    stacked = jnp.stack([east_speed, north_speed, ocean])
    static_ext = extended_2(stacked, (("gy", 2), ("gx", 3)), 1, True)
    position = lax.axis_index("gy")
    last_row = lax.axis_size("gy") - 1
    row_ids = lax.broadcasted_iota(jnp.int32, (rows_dev + 2, 1), 0)
    closed = (row_ids == 0) & (position == 0) | (row_ids == rows_dev + 1) & (position == last_row)
    row_keep = jnp.where(closed, 0.0, 1.0).astype(jnp.float32)
    ocean_ext = static_ext[2] * row_keep[None]
    current = tracer
    for section_index in range(TSTEPS):
        extended = extended_2(current, (("gy", 1), ("gx", 2)), 1, True)
        current = advect_block(extended, static_ext[0], static_ext[1], ocean_ext)
    forcing = surface_flux + jnp.sum(thickness[:, None, None] * ocean * current, axis=0)
    band_rhs, band_helm, band_wet = (
        lax.all_gather(forcing, "gx", axis=1, tiled=True),
        lax.all_gather(helm, "gx", axis=1, tiled=True),
        lax.all_gather(ocean_ext[0, :, 1:-1], "gx", axis=1, tiled=True),
    )
    wet_wrapped = wrap_columns(band_wet)
    band_diagonal = 6.0 + band_helm

    def apply_band(source):
        rimmed = extended_2(source, (("gy", 0),), 1, False)
        return stencil(wrap_columns(rimmed), wet_wrapped, band_diagonal)

    def sum_band(values):
        return lax.psum(values, "gy")

    band_heights = solve(band_rhs, band_diagonal, apply_band, sum_band)
    heights = lax.dynamic_slice_in_dim(band_heights, lax.axis_index("gx") * cols_dev, cols_dev, 1)
    return (current, heights)


def solution(mesh):
    in_specs = (
        P(None, "gy", "gx"),
        P(None, "gy", "gx"),
        P(None, "gy", "gx"),
        P("gy", "gx"),
        P(),
        P("gy", "gx"),
        P("gy", "gx"),
    )
    out_specs = (P(None, "gy", "gx"), P("gy", "gx"))
    return jax.shard_map(
        on_device, mesh=mesh, in_specs=in_specs, out_specs=out_specs, check_vma=False
    )
```

profile of v0, /device:TPU:0, one launch (start us, length us, event | category | flops | bytes accessed | tf_op | source)
XLA Modules:
  0.0 212.4 jit_solution(6373276697639543300)
XLA Ops:
  3.5 2.9 %collective-permute-start.1 = (f32[3,8,1,256]{3,2,1,0:T(1,128)S(1)}, f32[3,8,1,256]{3,2,1,0:T(1,128)S(1)}, u32[]{:S(2)}, u32[]{:S(2)}) collective-permute-start(f32[3,8,1,256]{3,2,1,0:T(1,128)S(1)} %get-tuple-element.27), channel_id=1, source_target_pairs={{4,0},{8,4},{12,8},{16,12},{20,16},{24,20},{28,24},{0,28},{5,1},{9... | collective-permute-start | bytes 73736 | tf_op jit(solution)/shard_map/ppermute | solution.py:18
  6.5 2.6 %collective-permute-start.5 = (f32[8,1,256]{2,1,0:T(1,128)S(1)}, f32[8,1,256]{2,1,0:T(1,128)S(1)}, u32[]{:S(2)}, u32[]{:S(2)}) collective-permute-start(f32[8,1,256]{2,1,0:T(1,128)S(1)} %get-tuple-element.34), channel_id=1, source_target_pairs={{4,0},{8,4},{12,8},{16,12},{20,16},{24,20},{28,24},{0,28},{5,1},{9... | collective-permute-start | bytes 24584 | tf_op jit(solution)/shard_map/ppermute | solution.py:18
  9.1 16.5 %all_gather.10 = f32[128,1024]{1,0:T(8,128)S(1)} all-gather(f32[128,256]{1,0:T(8,128)S(1)} %copy-done.16), channel_id=1, replica_groups=mesh['gy'=8,'gx'=4] {'gx'}, dimensions={1}, use_global_device_ids=true | all-gather | bytes 655360 | tf_op jit(solution)/shard_map/all_gather | solution.py:98
  29.3 3.1 %collective-permute-start.7 = (f32[8,130,1]{1,0,2:T(8,128)S(1)}, f32[8,130,1]{1,0,2:T(8,128)S(1)}, u32[]{:S(2)}, u32[]{:S(2)}) collective-permute-start(f32[8,130,1]{1,0,2:T(8,128)S(1)} %copy.29), channel_id=1, source_target_pairs={{1,0},{2,1},{3,2},{0,3},{5,4},{6,5},{7,6},{4,7},{9,8},{10,9},{11,1... | collective-permute-start | bytes 12488 | tf_op jit(solution)/shard_map/ppermute | solution.py:18
  32.4 1.9 pad_maximum_fusion.1
  34.3 2.2 %fusion.35 = (f32[3,8,130,1]{3,2,1,0:T(8,128)}, f32[3,8,130,1]{3,2,1,0:T(8,128)}) fusion(f32[3,8,130,256]{3,2,1,0:T(8,128)S(1)} %pad_maximum_fusion.1), kind=kLoop, calls=%fused_computation.108 | loop fusion | bytes 49920 | tf_op jit(solution)/shard_map/slice | solution.py:15
  36.5 2.3 %copy.23 = f32[3,8,130,1]{2,1,3,0:T(8,128)S(1)} copy(f32[3,8,130,1]{3,2,1,0:T(8,128)} %get-tuple-element.24) | data formatting | bytes 24960 | tf_op jit(solution)/shard_map/slice | solution.py:15
  38.9 2.3 %copy.24 = f32[3,8,130,1]{2,1,3,0:T(8,128)S(1)} copy(f32[3,8,130,1]{3,2,1,0:T(8,128)} %get-tuple-element.25) | data formatting | bytes 24960 | tf_op jit(solution)/shard_map/slice | solution.py:16
  41.2 3.8 %collective-permute-start.3 = (f32[3,8,130,1]{2,1,3,0:T(8,128)S(1)}, f32[3,8,130,1]{2,1,3,0:T(8,128)S(1)}, u32[]{:S(2)}, u32[]{:S(2)}) collective-permute-start(f32[3,8,130,1]{2,1,3,0:T(8,128)S(1)} %copy.24), channel_id=1, source_target_pairs={{1,0},{2,1},{3,2},{0,3},{5,4},{6,5},{7,6},{4,7},{9,8},{10,9},{11,1... | collective-permute-start | bytes 37448 | tf_op jit(solution)/shard_map/ppermute | solution.py:18
  47.2 1.8 copy.25
  49.0 1.8 copy.26
  50.8 5.7 %pad_maximum_fusion = f32[3,8,130,258]{3,2,1,0:T(8,128)S(1)} fusion(f32[3,8,130,1]{3,2,1,0:T(8,128)} %copy.26, f32[3,8,1,256]{3,2,1,0:T(1,128)S(1)} %collective-permute-done.1, f32[1,8,128,256]{3,2,1,0:T(8,128)S(1)} %fusion.15, f32[1,8,128,256]{3,2,1,0:T(8,128)} %bitcast.24, f32[1,8,128,256]{3,2,1,0:T(8,128)} %bitcast.28, ...), kind=kLoop, calls=%fused_computation | loop fusion | flops 4829760 | bytes 6439680 | tf_op jit(solution)/shard_map/concatenate | solution.py:19
  60.8 2.6 %collective-permute-start.9 = (f32[8,1,256]{2,1,0:T(1,128)S(1)}, f32[8,1,256]{2,1,0:T(1,128)S(1)}, u32[]{:S(2)}, u32[]{:S(2)}) collective-permute-start(f32[8,1,256]{2,1,0:T(1,128)S(1)} %get-tuple-element.32), channel_id=1, source_target_pairs={{4,0},{8,4},{12,8},{16,12},{20,16},{24,20},{28,24},{0,28},{5,1},{9... | collective-permute-start | bytes 24584 | tf_op jit(solution)/shard_map/ppermute | solution.py:18
  63.4 16.8 %all-gather = f32[1,130,1024]{2,1,0:T(8,128)} all-gather(f32[1,130,256]{2,1,0:T(8,128)S(1)} %slice.340), channel_id=2, replica_groups=mesh['gy'=8,'gx'=4] {'gx'}, dimensions={2}, use_global_device_ids=true | all-gather | bytes 665600 | tf_op jit(solution)/shard_map/all_gather | solution.py:99
  84.3 4.0 %collective-permute-start.11 = (f32[8,130,1]{1,0,2:T(8,128)S(1)}, f32[8,130,1]{1,0,2:T(8,128)S(1)}, u32[]{:S(2)}, u32[]{:S(2)}) collective-permute-start(f32[8,130,1]{1,0,2:T(8,128)S(1)} %copy.33), channel_id=1, source_target_pairs={{1,0},{2,1},{3,2},{0,3},{5,4},{6,5},{7,6},{4,7},{9,8},{10,9},{11,1... | collective-permute-start | bytes 12488 | tf_op jit(solution)/shard_map/ppermute | solution.py:18
  88.3 3.4 %fusion.12 = f32[8,129,256]{2,1,0:T(8,128)} fusion(f32[8,128,256]{2,1,0:T(8,128)S(1)} %fusion.14, f32[8,1,256]{2,1,0:T(1,128)S(1)} %collective-permute-done.8, f32[8,1,256]{2,1,0:T(1,128)S(1)} %collective-permute-done.9, f32[8,130,258]{2,1,0:T(8,128)} %copy-done.6, f32[8,130,258]{2,1,0:T(8,128)S(1)} %fusion), kind=kLoop, calls=%fused_computation.38 | loop fusion | flops 2377728 | bytes 5292032 | tf_op jit(solution)/shard_map/mul | solution.py:34
  93.8 3.0 %fusion.3 = f32[8,128,257]{2,1,0:T(8,128)S(1)} fusion(f32[8,130,1]{2,1,0:T(8,128)} %copy.34, f32[8,1,256]{2,1,0:T(1,128)S(1)} %collective-permute-done.9, f32[8,128,256]{2,1,0:T(8,128)S(1)} %fusion.14, f32[8,1,256]{2,1,0:T(1,128)S(1)} %collective-permute-done.8, f32[8,130,1]{2,1,0:T(8,128)} %copy.32, f32[8,130,258]{2,1,0:T(8,128)} %copy-done.3, ...), kind=kLoop, calls=%fused_computation.9 | loop fusion | flops 3421184 | bytes 5283968 | tf_op jit(solution)/shard_map/mul | solution.py:30
  96.8 1.5 multiply_reduce_fusion
  98.3 15.7 %all_gather.9 = f32[128,1024]{1,0:T(8,128)S(1)} all-gather(f32[128,256]{1,0:T(8,128)S(1)} %add.126), channel_id=1, replica_groups=mesh['gy'=8,'gx'=4] {'gx'}, dimensions={1}, use_global_device_ids=true | all-gather | bytes 655360 | tf_op jit(solution)/shard_map/all_gather | solution.py:97
  119.5 2.1 %concatenate.73 = f32[130,1026]{1,0:T(8,128)} concatenate(f32[130,1]{1,0:T(8,128)S(1)} %get-tuple-element.41, f32[130,1024]{1,0:T(8,128)} %copy-done.9, f32[130,1]{1,0:T(8,128)S(1)} %get-tuple-element.40), dimensions={1} | concatenate | bytes 1067040 | tf_op jit(solution)/shard_map/concatenate | solution.py:50
  124.2 16.0 %all-reduce.2 = (f32[]{:T(128)}, f32[]{:T(128)}) all-reduce(f32[]{:T(128)} %get-tuple-element.9, f32[]{:T(128)} %get-tuple-element.8), channel_id=1, replica_groups=mesh['gy'=8,'gx'=4] {'gy'}, use_global_device_ids=true, to_apply=%region_2.3 | all-reduce | flops 2 | bytes 16 | tf_op jit(solution)/shard_map/psum | solution.py:109
  141.8 1.4 collective-permute-start.14
  144.5 3.5 %collective-permute-done.15 = f32[1,1024]{1,0:T(1,128)S(1)} collective-permute-done((f32[1,1024]{1,0:T(1,128)S(1)}, f32[1,1024]{1,0:T(1,128)S(1)}, u32[]{:S(2)}, u32[]{:S(2)}) %collective-permute-start.15) | collective-permute-done | bytes 4128 | tf_op jit(solution)/shard_map/ppermute | solution.py:18
  149.0 2.1 %concatenate.75 = f32[130,1026]{1,0:T(8,128)} concatenate(f32[130,1]{1,0:T(8,128)S(1)} %get-tuple-element.39, f32[130,1024]{1,0:T(8,128)} %copy-done.10, f32[130,1]{1,0:T(8,128)S(1)} %get-tuple-element.38), dimensions={1} | concatenate | bytes 1067040 | tf_op jit(solution)/shard_map/concatenate | solution.py:50
  152.4 2.2 %multiply_reduce_fusion.2 = (f32[]{:T(128)}, f32[]{:T(128)}, f32[128,1024]{1,0:T(8,128)}) fusion(f32[128,1024]{1,0:T(8,128)S(1)} %copy-done.8, f32[128,1024]{1,0:T(8,128)S(1)} %all_gather.9, f32[128,1024]{1,0:T(8,128)S(1)} %get-tuple-element.19, f32[]{:T(128)S(6)} %div.31, f32[130,1026]{1,0:T(8,128)S(1)} %mul.198, f32[1,130,1024]{2,1,0:T(8,128)S(1)} %copy-done.2, ...), kind=kLoop, calls=%fused_computation.92 | loop fusion | flops 2359294 | bytes 7340044 | tf_op jit(solution)/shard_map/reduce_sum | solution.py:69
  154.6 16.6 %all-reduce.1 = (f32[]{:T(128)}, f32[]{:T(128)}) all-reduce(f32[]{:T(128)} %get-tuple-element.7, f32[]{:T(128)} %get-tuple-element.6), channel_id=1, replica_groups=mesh['gy'=8,'gx'=4] {'gy'}, use_global_device_ids=true, to_apply=%region_6.7 | all-reduce | flops 2 | bytes 16 | tf_op jit(solution)/shard_map/psum | solution.py:109
  176.1 2.1 add_divide_fusion
  179.0 1.4 collective-permute-start.16
  181.7 3.5 %collective-permute-done.17 = f32[1,1024]{1,0:T(1,128)S(1)} collective-permute-done((f32[1,1024]{1,0:T(1,128)S(1)}, f32[1,1024]{1,0:T(1,128)S(1)}, u32[]{:S(2)}, u32[]{:S(2)}) %collective-permute-start.17) | collective-permute-done | bytes 4128 | tf_op jit(solution)/shard_map/ppermute | solution.py:18
  188.7 1.4 fusion.21
  190.2 16.6 %all-reduce = (f32[]{:T(128)}, f32[]{:T(128)}) all-reduce(f32[]{:T(128)} %get-tuple-element.5, f32[]{:T(128)} %get-tuple-element.4), channel_id=1, replica_groups=mesh['gy'=8,'gx'=4] {'gy'}, use_global_device_ids=true, to_apply=%region_10.11 | all-reduce | flops 2 | bytes 16 | tf_op jit(solution)/shard_map/psum | solution.py:109
  210.7 1.7 fusion.31
  (106 shorter events, 36.3 us)
Async XLA Ops:
  0.6 1.3 copy-start.4
  1.9 4.5 %copy-start = (f32[8,128,256]{2,1,0:T(8,128)S(1)}, f32[8,128,256]{2,1,0:T(8,128)}, u32[]{:S(2)}) copy-start(f32[8,128,256]{2,1,0:T(8,128)} %param.7) | copy-start | bytes 3145732
  1.9 7.2 %copy-start.16 = (f32[128,256]{1,0:T(8,128)S(1)}, f32[128,256]{1,0:T(8,128)}, u32[]{:S(2)}) copy-start(f32[128,256]{1,0:T(8,128)} %param.13) | copy-start | bytes 393220
  2.9 29.5 %collective-permute-start = (f32[3,8,1,256]{3,2,1,0:T(1,128)S(1)}, f32[3,8,1,256]{3,2,1,0:T(1,128)S(1)}, u32[]{:S(2)}, u32[]{:S(2)}) collective-permute-start(f32[3,8,1,256]{3,2,1,0:T(1,128)S(1)} %get-tuple-element.26), channel_id=1, source_target_pairs={{0,4},{4,8},{8,12},{12,16},{16,20},{20,24},{24,28},{28,0},{1,5},{5... | collective-permute-start | bytes 73736 | tf_op jit(solution)/shard_map/ppermute | solution.py:17
  3.5 28.9 %collective-permute-start.1 = (f32[3,8,1,256]{3,2,1,0:T(1,128)S(1)}, f32[3,8,1,256]{3,2,1,0:T(1,128)S(1)}, u32[]{:S(2)}, u32[]{:S(2)}) collective-permute-start(f32[3,8,1,256]{3,2,1,0:T(1,128)S(1)} %get-tuple-element.27), channel_id=1, source_target_pairs={{4,0},{8,4},{12,8},{16,12},{20,16},{24,20},{28,24},{0,28},{5,1},{9... | collective-permute-start | bytes 73736 | tf_op jit(solution)/shard_map/ppermute | solution.py:18
  6.4 19.2 %collective-permute-start.4 = (f32[8,1,256]{2,1,0:T(1,128)S(1)}, f32[8,1,256]{2,1,0:T(1,128)S(1)}, u32[]{:S(2)}, u32[]{:S(2)}) collective-permute-start(f32[8,1,256]{2,1,0:T(1,128)S(1)} %get-tuple-element.35), channel_id=1, source_target_pairs={{0,4},{4,8},{8,12},{12,16},{16,20},{20,24},{24,28},{28,0},{1,5},{5... | collective-permute-start | bytes 24584 | tf_op jit(solution)/shard_map/ppermute | solution.py:17
  6.5 19.2 %collective-permute-start.5 = (f32[8,1,256]{2,1,0:T(1,128)S(1)}, f32[8,1,256]{2,1,0:T(1,128)S(1)}, u32[]{:S(2)}, u32[]{:S(2)}) collective-permute-start(f32[8,1,256]{2,1,0:T(1,128)S(1)} %get-tuple-element.34), channel_id=1, source_target_pairs={{4,0},{8,4},{12,8},{16,12},{20,16},{24,20},{28,24},{0,28},{5,1},{9... | collective-permute-start | bytes 24584 | tf_op jit(solution)/shard_map/ppermute | solution.py:18
  28.2 16.8 %collective-permute-start.6 = (f32[8,130,1]{1,0,2:T(8,128)S(1)}, f32[8,130,1]{1,0,2:T(8,128)S(1)}, u32[]{:S(2)}, u32[]{:S(2)}) collective-permute-start(f32[8,130,1]{1,0,2:T(8,128)S(1)} %copy.27), channel_id=1, source_target_pairs={{0,1},{1,2},{2,3},{3,0},{4,5},{5,6},{6,7},{7,4},{8,9},{9,10},{10,1... | collective-permute-start | bytes 12488 | tf_op jit(solution)/shard_map/ppermute | solution.py:17
  29.3 16.8 %collective-permute-start.7 = (f32[8,130,1]{1,0,2:T(8,128)S(1)}, f32[8,130,1]{1,0,2:T(8,128)S(1)}, u32[]{:S(2)}, u32[]{:S(2)}) collective-permute-start(f32[8,130,1]{1,0,2:T(8,128)S(1)} %copy.29), channel_id=1, source_target_pairs={{1,0},{2,1},{3,2},{0,3},{5,4},{6,5},{7,6},{4,7},{9,8},{10,9},{11,1... | collective-permute-start | bytes 12488 | tf_op jit(solution)/shard_map/ppermute | solution.py:18
  38.8 8.3 %collective-permute-start.2 = (f32[3,8,130,1]{2,1,3,0:T(8,128)S(1)}, f32[3,8,130,1]{2,1,3,0:T(8,128)S(1)}, u32[]{:S(2)}, u32[]{:S(2)}) collective-permute-start(f32[3,8,130,1]{2,1,3,0:T(8,128)S(1)} %copy.23), channel_id=1, source_target_pairs={{0,1},{1,2},{2,3},{3,0},{4,5},{5,6},{6,7},{7,4},{8,9},{9,10},{10,1... | collective-permute-start | bytes 37448 | tf_op jit(solution)/shard_map/ppermute | solution.py:17
  41.2 7.8 %collective-permute-start.3 = (f32[3,8,130,1]{2,1,3,0:T(8,128)S(1)}, f32[3,8,130,1]{2,1,3,0:T(8,128)S(1)}, u32[]{:S(2)}, u32[]{:S(2)}) collective-permute-start(f32[3,8,130,1]{2,1,3,0:T(8,128)S(1)} %copy.24), channel_id=1, source_target_pairs={{1,0},{2,1},{3,2},{0,3},{5,4},{6,5},{7,6},{4,7},{9,8},{10,9},{11,1... | collective-permute-start | bytes 37448 | tf_op jit(solution)/shard_map/ppermute | solution.py:18
  56.7 2.2 %copy-start.3 = (f32[8,130,258]{2,1,0:T(8,128)}, f32[8,130,258]{2,1,0:T(8,128)S(1)}, u32[]{:S(2)}) copy-start(f32[8,130,258]{2,1,0:T(8,128)S(1)} %get-tuple-element.22) | copy-start | bytes 3219844
  57.9 1.2 copy-start.13
  59.1 1.3 copy-start.1
  60.7 19.5 %collective-permute-start.8 = (f32[8,1,256]{2,1,0:T(1,128)S(1)}, f32[8,1,256]{2,1,0:T(1,128)S(1)}, u32[]{:S(2)}, u32[]{:S(2)}) collective-permute-start(f32[8,1,256]{2,1,0:T(1,128)S(1)} %get-tuple-element.33), channel_id=1, source_target_pairs={{0,4},{4,8},{8,12},{12,16},{16,20},{20,24},{24,28},{28,0},{1,5},{5... | collective-permute-start | bytes 24584 | tf_op jit(solution)/shard_map/ppermute | solution.py:17
  60.8 19.4 %collective-permute-start.9 = (f32[8,1,256]{2,1,0:T(1,128)S(1)}, f32[8,1,256]{2,1,0:T(1,128)S(1)}, u32[]{:S(2)}, u32[]{:S(2)}) collective-permute-start(f32[8,1,256]{2,1,0:T(1,128)S(1)} %get-tuple-element.32), channel_id=1, source_target_pairs={{4,0},{8,4},{12,8},{16,12},{20,16},{24,20},{28,24},{0,28},{5,1},{9... | collective-permute-start | bytes 24584 | tf_op jit(solution)/shard_map/ppermute | solution.py:18
  82.9 8.8 %collective-permute-start.10 = (f32[8,130,1]{1,0,2:T(8,128)S(1)}, f32[8,130,1]{1,0,2:T(8,128)S(1)}, u32[]{:S(2)}, u32[]{:S(2)}) collective-permute-start(f32[8,130,1]{1,0,2:T(8,128)S(1)} %copy.31), channel_id=1, source_target_pairs={{0,1},{1,2},{2,3},{3,0},{4,5},{5,6},{6,7},{7,4},{8,9},{9,10},{10,1... | collective-permute-start | bytes 12488 | tf_op jit(solution)/shard_map/ppermute | solution.py:17
  84.3 8.4 %collective-permute-start.11 = (f32[8,130,1]{1,0,2:T(8,128)S(1)}, f32[8,130,1]{1,0,2:T(8,128)S(1)}, u32[]{:S(2)}, u32[]{:S(2)}) collective-permute-start(f32[8,130,1]{1,0,2:T(8,128)S(1)} %copy.33), channel_id=1, source_target_pairs={{1,0},{2,1},{3,2},{0,3},{5,4},{6,5},{7,6},{4,7},{9,8},{10,9},{11,1... | collective-permute-start | bytes 12488 | tf_op jit(solution)/shard_map/ppermute | solution.py:18
  93.8 3.0 %copy-start.5 = (f32[8,129,256]{2,1,0:T(8,128)S(1)}, f32[8,129,256]{2,1,0:T(8,128)}, u32[]{:S(2)}) copy-start(f32[8,129,256]{2,1,0:T(8,128)} %fusion.12) | copy-start | bytes 3170308
  93.8 3.0 %copy-start.15 = (s32[128,256]{1,0:T(8,128)S(1)}, s32[128,256]{1,0:T(8,128)}, u32[]{:S(2)}) copy-start(s32[128,256]{1,0:T(8,128)} %param.10) | copy-start | bytes 393220
  93.8 3.0 %copy-start.18 = (f32[8]{0:T(128)S(1)}, f32[8]{0:T(128)}, u32[]{:S(2)}) copy-start(f32[8]{0:T(128)} %param.11) | copy-start | bytes 100
  96.8 1.5 copy-start.17
  98.3 18.5 %copy-start.2 = (f32[1,130,1024]{2,1,0:T(8,128)S(1)}, f32[1,130,1024]{2,1,0:T(8,128)}, u32[]{:S(2)}) copy-start(f32[1,130,1024]{2,1,0:T(8,128)} %all-gather) | copy-start | bytes 1597444
  114.2 3.1 %collective-permute-start.12 = (f32[1,1024]{1,0:T(1,128)S(1)}, f32[1,1024]{1,0:T(1,128)S(1)}, u32[]{:S(2)}, u32[]{:S(2)}) collective-permute-start(f32[1,1024]{1,0:T(1,128)S(1)} %get-tuple-element.48), channel_id=1, source_target_pairs={{0,4},{4,8},{8,12},{12,16},{16,20},{20,24},{24,28},{1,5},{5,9},{9,... | collective-permute-start | bytes 12296 | tf_op jit(solution)/shard_map/ppermute | solution.py:17
  115.5 3.1 %collective-permute-start.13 = (f32[1,1024]{1,0:T(1,128)S(1)}, f32[1,1024]{1,0:T(1,128)S(1)}, u32[]{:S(2)}, u32[]{:S(2)}) collective-permute-start(f32[1,1024]{1,0:T(1,128)S(1)} %get-tuple-element.49), channel_id=1, source_target_pairs={{4,0},{8,4},{12,8},{16,12},{20,16},{24,20},{28,24},{5,1},{9,5},{13... | collective-permute-start | bytes 12296 | tf_op jit(solution)/shard_map/ppermute | solution.py:18
  141.8 6.3 %copy-start.7 = (f32[128,1024]{1,0:T(8,128)}, f32[128,1024]{1,0:T(8,128)S(1)}, u32[]{:S(2)}) copy-start(f32[128,1024]{1,0:T(8,128)S(1)} %add_divide_fusion.1) | copy-start | bytes 1572868
  141.8 2.7 %collective-permute-start.14 = (f32[1,1024]{1,0:T(1,128)S(1)}, f32[1,1024]{1,0:T(1,128)S(1)}, u32[]{:S(2)}, u32[]{:S(2)}) collective-permute-start(f32[1,1024]{1,0:T(1,128)S(1)} %get-tuple-element.46), channel_id=1, source_target_pairs={{0,4},{4,8},{8,12},{12,16},{16,20},{20,24},{24,28},{1,5},{5,9},{9,... | collective-permute-start | bytes 12296 | tf_op jit(solution)/shard_map/ppermute | solution.py:17
  143.2 4.8 %collective-permute-start.15 = (f32[1,1024]{1,0:T(1,128)S(1)}, f32[1,1024]{1,0:T(1,128)S(1)}, u32[]{:S(2)}, u32[]{:S(2)}) collective-permute-start(f32[1,1024]{1,0:T(1,128)S(1)} %get-tuple-element.47), channel_id=1, source_target_pairs={{4,0},{8,4},{12,8},{16,12},{20,16},{24,20},{28,24},{5,1},{9,5},{13... | collective-permute-start | bytes 12296 | tf_op jit(solution)/shard_map/ppermute | solution.py:18
  151.2 1.2 copy-start.8
  179.0 2.7 %collective-permute-start.16 = (f32[1,1024]{1,0:T(1,128)S(1)}, f32[1,1024]{1,0:T(1,128)S(1)}, u32[]{:S(2)}, u32[]{:S(2)}) collective-permute-start(f32[1,1024]{1,0:T(1,128)S(1)} %get-tuple-element.44), channel_id=1, source_target_pairs={{0,4},{4,8},{8,12},{12,16},{16,20},{20,24},{24,28},{1,5},{5,9},{9,... | collective-permute-start | bytes 12296 | tf_op jit(solution)/shard_map/ppermute | solution.py:17
  180.4 4.8 %collective-permute-start.17 = (f32[1,1024]{1,0:T(1,128)S(1)}, f32[1,1024]{1,0:T(1,128)S(1)}, u32[]{:S(2)}, u32[]{:S(2)}) collective-permute-start(f32[1,1024]{1,0:T(1,128)S(1)} %get-tuple-element.45), channel_id=1, source_target_pairs={{4,0},{8,4},{12,8},{16,12},{20,16},{24,20},{28,24},{5,1},{9,5},{13... | collective-permute-start | bytes 12296 | tf_op jit(solution)/shard_map/ppermute | solution.py:18
  187.5 1.2 copy-start.14
  (5 other events, 4.7 us)
where the time goes:
time: 215 us; the launch traced here: 212 us
  blocking collectives  98.3 us (46%)
  other arithmetic  34.3 us (16%)
  local copies, waits for them, and re-layouts  31.6 us (15%)
  starting transfers between devices  28.6 us (13%)
  between operations  11.2 us (5%)
  waiting for transfers between devices  8.4 us (4%)
    psum x3, blocking collectives, sum_band(): return lax.psum(values, 'gy')  49.2 us
    ppermute x9, starting transfers between devices, extended_2(): after = lax.ppermute(first, axis, down)  23 us
    all_gather x1, blocking collectives, on_device(): lax.all_gather(ocean_ext[0, :, 1:-1], 'gx', axis=1, tiled=True)  16.8 us
    all_gather x1, blocking collectives, on_device(): lax.all_gather(helm, 'gx', axis=1, tiled=True)  16.5 us
    all_gather x1, blocking collectives, on_device(): lax.all_gather(forcing, 'gx', axis=1, tiled=True)  15.7 us
    slice x9, local copies, waits for them, and re-layouts, extended_2(): last = lax.slice_in_dim(array, length - width, length, axis=dim)  9.51 us
    concatenate x7, other arithmetic, extended_2(): array = jnp.concatenate([before, array, after], axis=dim)  8.98 us
    ppermute x9, waiting for transfers between devices, extended_2(): after = lax.ppermute(first, axis, down)  8.37 us
  transfers between devices with their start and end apart: 18, of which 3 were waited for; matrix products, arithmetic and copies ran while one was open for 10% of the time, Pallas kernels for 0%

commit v1 on v0

v1 whole, which is shorter than its diff:
```python
import functools

import jax
import jax.numpy as jnp
from jax import lax
from jax.experimental import pallas as pl
from jax.experimental.pallas import tpu as pltpu
from jax.sharding import PartitionSpec as P

TSTEPS = 2
ITERS = 3
MESH = pl.DeviceIdType.MESH
SUB = 8
LANE = 128
AROUND = ((1, 0), (-1, 0), (0, 1), (0, -1), (1, 1), (1, -1), (-1, 1), (-1, -1))


def roll(array, shift, axis):
    shift = shift % array.shape[axis]
    return pltpu.roll(array, shift, axis) if shift else array


def iota(shape, dim):
    return lax.broadcasted_iota(jnp.int32, shape, dim)


def kernel(
    ny,
    nx,
    tracer_ref,
    east_ref,
    north_ref,
    columns_ref,
    thickness_ref,
    surface_ref,
    helm_ref,
    tracer_out,
    heights_out,
    c_ext,
    e_ext,
    n_ext,
    col_in,
    surf_in,
    flat_ext,
    pack,
    pack_recv,
    corner_recv,
    up_send,
    down_send,
    up_recv,
    down_recv,
    forcing,
    start_vec,
    flat_pack,
    edge_pack,
    row_recv,
    edge_recv,
    edge_corner_recv,
    part,
    slots,
    in_sem,
    out_sem,
    send_sem,
    recv_sem,
    sum_send_sem,
    sum_recv_sem,
):
    levels, rows, cols = tracer_ref.shape
    ext_rows, ext_cols = rows + SUB, cols + LANE
    my_y, my_x = lax.axis_index("gy"), lax.axis_index("gx")
    count = ny * nx
    my_id = my_y * nx + my_x

    def place(offset):
        target = lax.rem(my_id + offset, count)
        return (target // nx, lax.rem(target, nx))

    def near(dy, dx):
        return (lax.rem(my_y + dy + ny, ny), lax.rem(my_x + dx + nx, nx))

    loads = [
        pltpu.make_async_copy(columns_ref, col_in, in_sem.at[0]),
        pltpu.make_async_copy(helm_ref, flat_ext.at[1, 0:rows, 0:cols], in_sem.at[1]),
        pltpu.make_async_copy(tracer_ref, c_ext.at[:, 0:rows, 0:cols], in_sem.at[2]),
        pltpu.make_async_copy(east_ref, e_ext.at[:, 0:rows, 0:cols], in_sem.at[3]),
        pltpu.make_async_copy(north_ref, n_ext.at[:, 0:rows, 0:cols], in_sem.at[4]),
        pltpu.make_async_copy(surface_ref, surf_in, in_sem.at[5]),
    ]
    for load in loads:
        load.start()
    barrier = pltpu.get_barrier_semaphore()
    for offset in range(1, count):
        pl.semaphore_signal(barrier, inc=1, device_id=place(offset), device_id_type=MESH)
    for load in loads:
        load.wait()

    fields = (c_ext, e_ext, n_ext)
    flat_ext[0, 0:rows, 0:cols] = col_in[...].astype(jnp.float32)

    lane_full = iota((rows, LANE), 1)
    lane_half = lane_full < LANE // 2
    group = ((lane_full + 2) % LANE) // 4

    def both_edges(ref, index):
        return jnp.where(lane_half, ref[index, 0:rows, 0:LANE], ref[index, 0:rows, cols - LANE : cols])

    sources = [(fields[f], k, f) for k in range(levels) for f in range(3)]
    sources += [(flat_ext, 0, 3), (flat_ext, 1, 4)]
    packed = jnp.zeros((rows, LANE), jnp.float32)
    for slot, (ref, index, _) in enumerate(sources):
        packed = jnp.where(group == slot, roll(both_edges(ref, index), 4 * slot, 1), packed)
    pack[...] = packed

    sub = iota((SUB, cols), 0)
    for k in range(levels):
        quads = [(ref, k) for ref in fields] + [(flat_ext, min(k, 1))]
        up = jnp.zeros((SUB, cols), jnp.float32)
        down = jnp.zeros((SUB, cols), jnp.float32)
        for f, (ref, index) in enumerate(quads):
            mine = sub // 2 == f
            up = jnp.where(mine, roll(ref[index, rows - SUB : rows, 0:cols], 2 * f + 2, 0), up)
            down = jnp.where(mine, roll(ref[index, 0:SUB, 0:cols], 2 * f, 0), down)
        up_send[k] = up
        down_send[k] = down

    pl.semaphore_wait(barrier, count - 1)

    first_rows, last_rows = pl.ds(0, SUB), pl.ds(rows - SUB, SUB)
    first = [
        (up_send, up_recv),
        (down_send, down_recv),
        (pack, pack_recv.at[0]),
        (pack, pack_recv.at[1]),
        (pack.at[last_rows], corner_recv.at[0]),
        (pack.at[last_rows], corner_recv.at[1]),
        (pack.at[first_rows], corner_recv.at[2]),
        (pack.at[first_rows], corner_recv.at[3]),
    ]

    def exchange(pairs, base):
        copies = []
        for which, (source, target) in enumerate(pairs):
            copies.append(
                pltpu.make_async_remote_copy(
                    src_ref=source,
                    dst_ref=target,
                    send_sem=send_sem.at[base + which],
                    recv_sem=recv_sem.at[base + which],
                    device_id=near(*AROUND[which]),
                    device_id_type=MESH,
                )
            )
        for copy in copies:
            copy.start()
        return copies

    copies = exchange(first, 0)
    for copy in copies:
        copy.wait_recv()

    from_right = (iota((rows, LANE), 1) % 4) < 2
    sides = jnp.where(from_right, pack_recv[1], pack_recv[0])
    small_right = (iota((SUB, LANE), 1) % 4) < 2
    small_below = iota((SUB, LANE), 0) < SUB // 2
    south = jnp.where(small_right, corner_recv[1], corner_recv[0])
    north = jnp.where(small_right, corner_recv[3], corner_recv[2])
    corner = jnp.where(small_below, north, south)
    for slot, (ref, index, _) in enumerate(sources):
        ref[index, 0:rows, cols:ext_cols] = roll(sides, -4 * slot, 1)
        ref[index, rows:ext_rows, cols:ext_cols] = roll(corner, -4 * slot, 1)
    for k in range(levels):
        quads = [(ref, k) for ref in fields] + ([(flat_ext, k)] if k < 2 else [])
        for f, (ref, index) in enumerate(quads):
            ref[index, rows:ext_rows, 0:cols] = jnp.where(
                sub < SUB // 2,
                roll(down_recv[k], -2 * f, 0),
                roll(up_recv[k], -2 * f - 2, 0),
            )

    row_ids = iota((SUB, ext_cols), 0)
    beyond = (row_ids >= SUB // 2) & (my_y == 0) | (row_ids < SUB // 2) & (my_y == ny - 1)
    flat_ext[0, rows:ext_rows] = jnp.where(beyond, 0.0, flat_ext[0, rows:ext_rows])

    forcing[...] = surf_in[...]

    def level(k, carry):
        depth = flat_ext[0]
        ocean = jnp.where(depth > lax.convert_element_type(k, jnp.float32), 1.0, 0.0)
        east = e_ext[k] * (ocean * roll(ocean, -1, 1))
        nort = n_ext[k] * (ocean * roll(ocean, -1, 0))
        current = c_ext[k]
        for _ in range(TSTEPS):
            flux_east = jnp.maximum(east, 0.0) * current + jnp.minimum(east, 0.0) * roll(
                current, -1, 1
            )
            flux_north = jnp.maximum(nort, 0.0) * current + jnp.minimum(nort, 0.0) * roll(
                current, -1, 0
            )
            current = current - (
                flux_east - roll(flux_east, 1, 1) + flux_north - roll(flux_north, 1, 0)
            )
        c_ext[k] = current
        forcing[...] += (thickness_ref[k] * ocean * current)[0:rows, 0:cols]
        return carry

    lax.fori_loop(0, levels, level, 0)

    out_copy = pltpu.make_async_copy(c_ext.at[:, 0:rows, 0:cols], tracer_out, out_sem)
    out_copy.start()

    diagonal = 6.0 + flat_ext[1, 0:rows, 0:cols]
    wet = jnp.where(flat_ext[0, 0:rows, 0:cols] > 0.0, 1.0, 0.0)
    z0 = forcing[...] / diagonal
    y0 = wet * z0
    start_vec[0:rows, 0:cols] = y0
    edges = jnp.where(lane_half, y0[:, 0:LANE], y0[:, cols - LANE : cols])
    flat_pack[...] = edges
    edge_pack[...] = edges.T
    last_lanes = pl.ds(LANE - SUB, SUB)
    second = [
        (start_vec.at[last_rows, pl.ds(0, cols)], row_recv.at[0]),
        (start_vec.at[first_rows, pl.ds(0, cols)], row_recv.at[1]),
        (edge_pack.at[last_lanes], edge_recv.at[0]),
        (edge_pack.at[first_rows], edge_recv.at[1]),
        (flat_pack.at[last_rows], edge_corner_recv.at[0]),
        (flat_pack.at[last_rows], edge_corner_recv.at[1]),
        (flat_pack.at[first_rows], edge_corner_recv.at[2]),
        (flat_pack.at[first_rows], edge_corner_recv.at[3]),
    ]
    more = exchange(second, len(AROUND))
    for copy in more:
        copy.wait_recv()

    turned = jnp.concatenate(
        [edge_recv[1], jnp.zeros((LANE - 2 * SUB, rows), jnp.float32), edge_recv[0]], axis=0
    )
    lane_small = iota((SUB, LANE), 1) < LANE // 2
    south = jnp.where(lane_small, edge_corner_recv[1], edge_corner_recv[0])
    north = jnp.where(lane_small, edge_corner_recv[3], edge_corner_recv[2])
    for copy in more:
        copy.wait_send()
    start_vec[0:rows, cols:ext_cols] = turned.T
    start_vec[rows:ext_rows, cols:ext_cols] = jnp.where(small_below, north, south)
    start_vec[rows:ext_rows, 0:cols] = jnp.where(sub < SUB // 2, row_recv[1], row_recv[0])
    start_vec[rows:ext_rows] = jnp.where(beyond, 0.0, start_vec[rows:ext_rows])

    scale = jnp.where(flat_ext[0] > 0.0, 1.0 / (6.0 + flat_ext[1]), 0.0)

    def off_diagonal(vector):
        across = roll(vector, 1, 1) + roll(vector, -1, 1)
        mixed = vector + 0.5 * across
        return scale * (across + roll(mixed, 1, 0) + roll(mixed, -1, 0))

    z1_ext = off_diagonal(start_vec[...])
    z2_ext = off_diagonal(z1_ext)
    z3_ext = off_diagonal(z2_ext)
    z1, z2, z3 = (z[0:rows, 0:cols] for z in (z1_ext, z2_ext, z3_ext))

    def partial(values):
        folded = jnp.sum(values, axis=0, keepdims=True)
        return sum(folded[:, i : i + LANE] for i in range(0, cols, LANE))

    d0, d1, d2 = (diagonal * z for z in (z0, z1, z2))
    sums = [partial(v) for v in (d0 * z0, d0 * z1, d1 * z1, d1 * z2, d2 * z2, d2 * z3)]
    part[...] = jnp.concatenate(sums + [jnp.zeros((SUB - len(sums), LANE), jnp.float32)], axis=0)

    for offset in range(1, count):
        pltpu.make_async_remote_copy(
            src_ref=part,
            dst_ref=slots.at[offset - 1],
            send_sem=sum_send_sem,
            recv_sem=sum_recv_sem,
            device_id=place(offset),
            device_id_type=MESH,
        ).start()
    everything = pltpu.make_async_remote_copy(
        src_ref=slots,
        dst_ref=slots,
        send_sem=sum_send_sem,
        recv_sem=sum_recv_sem,
        device_id=place(1),
        device_id_type=MESH,
    )
    everything.wait_recv()
    total = jnp.sum(jnp.sum(slots[...], axis=0) + part[...], axis=1, keepdims=True)
    moment = [total[i : i + 1, :] for i in range(2 * ITERS)]

    def inner(a, b):
        return sum(x * y * moment[i + j] for i, x in enumerate(a) for j, y in enumerate(b))

    def ratio(top, bottom):
        good = bottom > 0.0
        return jnp.where(good, top / jnp.where(good, bottom, 1.0), 0.0)

    one, zero = jnp.ones((1, 1), jnp.float32), jnp.zeros((1, 1), jnp.float32)
    scaled, direction, height = [one], [one], [zero] * ITERS
    product_now = moment[0]
    for iteration in range(ITERS):
        low, high = direction + [zero], [zero] + direction
        applied = [a - b for a, b in zip(low, high)]
        step_size = ratio(product_now, inner(direction, applied))
        for i, x in enumerate(direction):
            height[i] = height[i] + step_size * x
        if iteration + 1 < ITERS:
            scaled = [a - step_size * b for a, b in zip(scaled + [zero], applied)]
            product_next = jnp.maximum(inner(scaled, scaled), 0.0)
            factor = ratio(product_next, product_now)
            direction = [a + factor * b for a, b in zip(scaled, low)]
            product_now = product_next
    heights_out[...] = height[0] * z0 + height[1] * z1 + height[2] * z2

    everything.wait_send()
    for copy in copies:
        copy.wait_send()
    out_copy.wait()


def on_device(ny, nx, tracer, east_speed, north_speed, columns, thickness, surface_flux, helm):
    levels, rows, cols = tracer.shape
    ext = (rows + SUB, cols + LANE)
    hbm = pl.BlockSpec(memory_space=pl.ANY)
    vmem = pl.BlockSpec(memory_space=pltpu.VMEM)
    smem = pl.BlockSpec(memory_space=pltpu.SMEM)
    f32 = jnp.float32
    dma = pltpu.SemaphoreType.DMA
    scratch = [
        pltpu.VMEM((levels, *ext), f32),
        pltpu.VMEM((levels, *ext), f32),
        pltpu.VMEM((levels, *ext), f32),
        pltpu.VMEM((rows, cols), jnp.int32),
        pltpu.VMEM((rows, cols), f32),
        pltpu.VMEM((2, *ext), f32),
        pltpu.VMEM((rows, LANE), f32),
        pltpu.VMEM((2, rows, LANE), f32),
        pltpu.VMEM((4, SUB, LANE), f32),
        pltpu.VMEM((levels, SUB, cols), f32),
        pltpu.VMEM((levels, SUB, cols), f32),
        pltpu.VMEM((levels, SUB, cols), f32),
        pltpu.VMEM((levels, SUB, cols), f32),
        pltpu.VMEM((rows, cols), f32),
        pltpu.VMEM(ext, f32),
        pltpu.VMEM((rows, LANE), f32),
        pltpu.VMEM((LANE, rows), f32),
        pltpu.VMEM((2, SUB, cols), f32),
        pltpu.VMEM((2, SUB, rows), f32),
        pltpu.VMEM((4, SUB, LANE), f32),
        pltpu.VMEM((SUB, LANE), f32),
        pltpu.VMEM((ny * nx - 1, SUB, LANE), f32),
        dma((6,)),
        dma,
        dma((2 * len(AROUND),)),
        dma((2 * len(AROUND),)),
        dma,
        dma,
    ]
    return pl.pallas_call(
        functools.partial(kernel, ny, nx),
        out_shape=(
            jax.ShapeDtypeStruct((levels, rows, cols), f32),
            jax.ShapeDtypeStruct((rows, cols), f32),
        ),
        in_specs=[hbm, hbm, hbm, hbm, smem, hbm, hbm],
        out_specs=(hbm, vmem),
        scratch_shapes=scratch,
        compiler_params=pltpu.CompilerParams(collective_id=0, has_side_effects=True),
    )(tracer, east_speed, north_speed, columns, thickness, surface_flux, helm)


def solution(mesh):
    spec = P(None, "gy", "gx")
    flat = P("gy", "gx")
    return jax.shard_map(
        functools.partial(on_device, mesh.shape["gy"], mesh.shape["gx"]),
        mesh=mesh,
        in_specs=(spec, spec, spec, flat, P(), flat, flat),
        out_specs=(spec, flat),
        check_vma=False,
    )
```

time: 215 us -> 32.9 us (0.15); the launches traced: 212 us -> 32.7 us
  blocking collectives: 98.3 us -> 0 us
  other arithmetic: 34.3 us -> 0 us
  Pallas kernels: 0 us -> 29.1 us
  local copies, waits for them, and re-layouts: 31.6 us -> 2.96 us
  starting transfers between devices: 28.6 us -> 0 us
  between operations: 11.2 us -> 0.65 us
  waiting for transfers between devices: 8.4 us -> 0 us
    psum x3 -> x0, blocking collectives: 49.2 us -> none  [sum_band(): return lax.psum(values, 'gy')]
    all_gather x3 -> x0, blocking collectives: 49 us -> none  [the longest x1 16.8 us: on_device(): lax.all_gather(ocean_ext[0, :, 1:-1], 'gx', axis=1, tiled=True)]
    pallas_call x0 -> x1, Pallas kernels: none -> 29.1 us  [on_device(): pl.pallas_call(functools.partial(kernel, ny, nx), out_shape=(jax.ShapeDty...]
    ppermute x18 -> x0, starting transfers between devices: 28.6 us -> none  [the longest x9 23 us: extended_2(): after = lax.ppermute(first, axis, down)]
    slice x19 -> x0, local copies, waits for them, and re-layouts: 14 us -> none  [the longest x9 9.51 us: extended_2(): last = lax.slice_in_dim(array, length - width, length, axis=dim)]
    mul x8 -> x0, other arithmetic: 12.3 us -> none  [the longest x2 4.35 us: advect_block(): open_north * upwind(north_ext[:, :-1, 1:-1], extended[:, :-1, 1:-1], exte...]
    concatenate x7 -> x0, other arithmetic: 8.98 us -> none  [extended_2(): array = jnp.concatenate([before, array, after], axis=dim)]
    ppermute x18 -> x0, waiting for transfers between devices: 8.4 us -> none  [the longest x9 8.37 us: extended_2(): after = lax.ppermute(first, axis, down)]
  transfers between devices with their start and end apart: 18 -> 0, of which waited for: 3 -> 0; matrix products, arithmetic and copies ran while one was open for 10% -> 0% of each run, Pallas kernels for 0% -> 0%
where the time goes in v1:
time: 32.9 us; the launch traced here: 32.7 us
  Pallas kernels  29.1 us (88%)
  local copies, waits for them, and re-layouts  2.96 us (9%)
  between operations  0.65 us (2%)
    pallas_call x1, Pallas kernels, on_device(): pl.pallas_call(functools.partial(kernel, ny, nx), out_shape=(jax.ShapeDty...  29.1 us
    unnamed x4, local copies, waits for them, and re-layouts  2.96 us

profile of v1, /device:TPU:0, one launch (start us, length us, event | category | flops | bytes accessed | tf_op | source)
XLA Modules:
  0.0 32.7 jit_solution(4785212251648355570)
XLA Ops:
  0.6 29.1 %shard_map.86 = (f32[8,128,256]{2,1,0:T(8,128)}, f32[128,256]{1,0:T(8,128)}) custom-call(f32[8,128,256]{2,1,0:T(8,128)} %tracer_ref.1, f32[8,128,256]{2,1,0:T(8,128)} %east_ref.1, f32[8,128,256]{2,1,0:T(8,128)} %north_ref.1, s32[128,256]{1,0:T(8,128)} %columns_ref.1, f32[8]{0:T(128)} %thickness_ref.1, f32[128,256]{1,0:T(8,128)} %surface_ref.1, ...), custom_call_target="tpu_custom_call" | custom-call | tf_op jit(solution)/shard_map/pallas_call | solution.py:356
  29.8 0.0 copy-start
  29.8 2.3 %copy.11 = f32[8,128,256]{2,1,0:T(8,128)} copy(f32[8,128,256]{2,1,0:T(8,128)} %get-tuple-element.4) | data formatting | bytes 2097152
  32.1 0.0 copy-done
  32.1 0.7 %copy.12 = f32[128,256]{1,0:T(8,128)} copy(f32[128,256]{1,0:T(8,128)S(1)} %copy-done) | data formatting | bytes 262144
Async XLA Ops:
  29.8 2.3 %copy-start = (f32[128,256]{1,0:T(8,128)S(1)}, f32[128,256]{1,0:T(8,128)}, u32[]{:S(2)}) copy-start(f32[128,256]{1,0:T(8,128)} %get-tuple-element.5) | copy-start | bytes 393220

commit v2 on v1

--- a/solution.py
+++ b/solution.py
@@ -42,8 +42,12 @@
     col_in,
     surf_in,
     flat_ext,
+    face_levels,
     pack,
-    pack_recv,
+    to_left,
+    to_right,
+    from_left,
+    from_right,
     corner_recv,
     up_send,
     down_send,
@@ -99,7 +103,7 @@
 
     lane_full = iota((rows, LANE), 1)
     lane_half = lane_full < LANE // 2
-    group = ((lane_full + 2) % LANE) // 4
+    group = lane_full // 4
 
     def both_edges(ref, index):
         return jnp.where(lane_half, ref[index, 0:rows, 0:LANE], ref[index, 0:rows, cols - LANE : cols])
@@ -108,8 +112,14 @@
     sources += [(flat_ext, 0, 3), (flat_ext, 1, 4)]
     packed = jnp.zeros((rows, LANE), jnp.float32)
     for slot, (ref, index, _) in enumerate(sources):
-        packed = jnp.where(group == slot, roll(both_edges(ref, index), 4 * slot, 1), packed)
+        packed = jnp.where(group == slot, roll(both_edges(ref, index), 4 * slot + 2, 1), packed)
     pack[...] = packed
+    turned = packed.T
+    sub_rows = iota((SUB, rows), 0) % 4 < 2
+    for p in range(to_left.shape[0]):
+        one, two = turned[2 * SUB * p :][:SUB], turned[2 * SUB * p + SUB :][:SUB]
+        to_right[p] = jnp.where(sub_rows, one, roll(two, 2, 0))
+        to_left[p] = jnp.where(sub_rows, roll(two, -2, 0), one)
 
     sub = iota((SUB, cols), 0)
     for k in range(levels):
@@ -129,8 +139,8 @@
     first = [
         (up_send, up_recv),
         (down_send, down_recv),
-        (pack, pack_recv.at[0]),
-        (pack, pack_recv.at[1]),
+        (to_right, from_left),
+        (to_left, from_right),
         (pack.at[last_rows], corner_recv.at[0]),
         (pack.at[last_rows], corner_recv.at[1]),
         (pack.at[first_rows], corner_recv.at[2]),
@@ -158,16 +168,23 @@
     for copy in copies:
         copy.wait_recv()
 
-    from_right = (iota((rows, LANE), 1) % 4) < 2
-    sides = jnp.where(from_right, pack_recv[1], pack_recv[0])
-    small_right = (iota((SUB, LANE), 1) % 4) < 2
+    pieces = []
+    for p in range(to_left.shape[0]):
+        x, y = from_left[p], from_right[p]
+        pieces.append(jnp.where(sub_rows, x, y))
+        pieces.append(jnp.where(sub_rows, roll(x, -2, 0), roll(y, 2, 0)))
+    spare = LANE - 2 * SUB * to_left.shape[0]
+    if spare:
+        pieces.append(jnp.zeros((spare, rows), jnp.float32))
+    sides = jnp.concatenate(pieces, axis=0).T
+    small_right = (iota((SUB, LANE), 1) % 4) >= 2
     small_below = iota((SUB, LANE), 0) < SUB // 2
     south = jnp.where(small_right, corner_recv[1], corner_recv[0])
     north = jnp.where(small_right, corner_recv[3], corner_recv[2])
     corner = jnp.where(small_below, north, south)
     for slot, (ref, index, _) in enumerate(sources):
-        ref[index, 0:rows, cols:ext_cols] = roll(sides, -4 * slot, 1)
-        ref[index, rows:ext_rows, cols:ext_cols] = roll(corner, -4 * slot, 1)
+        ref[index, 0:rows, cols:ext_cols] = roll(sides, -4 * slot - 2, 1)
+        ref[index, rows:ext_rows, cols:ext_cols] = roll(corner, -4 * slot - 2, 1)
     for k in range(levels):
         quads = [(ref, k) for ref in fields] + ([(flat_ext, k)] if k < 2 else [])
         for f, (ref, index) in enumerate(quads):
@@ -183,24 +200,24 @@
 
     forcing[...] = surf_in[...]
 
+    depth = flat_ext[0]
+    face_levels[0] = jnp.minimum(depth, roll(depth, -1, 1))
+    face_levels[1] = jnp.minimum(depth, roll(depth, -1, 0))
+
     def level(k, carry):
-        depth = flat_ext[0]
-        ocean = jnp.where(depth > lax.convert_element_type(k, jnp.float32), 1.0, 0.0)
-        east = e_ext[k] * (ocean * roll(ocean, -1, 1))
-        nort = n_ext[k] * (ocean * roll(ocean, -1, 0))
+        below = lax.convert_element_type(k, jnp.float32)
+        east = jnp.where(face_levels[0] > below, e_ext[k], 0.0)
+        nort = jnp.where(face_levels[1] > below, n_ext[k], 0.0)
         current = c_ext[k]
         for _ in range(TSTEPS):
-            flux_east = jnp.maximum(east, 0.0) * current + jnp.minimum(east, 0.0) * roll(
-                current, -1, 1
-            )
-            flux_north = jnp.maximum(nort, 0.0) * current + jnp.minimum(nort, 0.0) * roll(
-                current, -1, 0
-            )
+            flux_east = east * jnp.where(east > 0.0, current, roll(current, -1, 1))
+            flux_north = nort * jnp.where(nort > 0.0, current, roll(current, -1, 0))
             current = current - (
                 flux_east - roll(flux_east, 1, 1) + flux_north - roll(flux_north, 1, 0)
             )
         c_ext[k] = current
-        forcing[...] += (thickness_ref[k] * ocean * current)[0:rows, 0:cols]
+        open_here = flat_ext[0, 0:rows, 0:cols] > below
+        forcing[...] += jnp.where(open_here, thickness_ref[k] * current[0:rows, 0:cols], 0.0)
         return carry
 
     lax.fori_loop(0, levels, level, 0)
@@ -262,7 +279,11 @@
 
     d0, d1, d2 = (diagonal * z for z in (z0, z1, z2))
     sums = [partial(v) for v in (d0 * z0, d0 * z1, d1 * z1, d1 * z2, d2 * z2, d2 * z3)]
-    part[...] = jnp.concatenate(sums + [jnp.zeros((SUB - len(sums), LANE), jnp.float32)], axis=0)
+    folded = jnp.concatenate(sums + [jnp.zeros((SUB - len(sums), LANE), jnp.float32)], axis=0)
+    for shift in (64, 32, 16):
+        folded = folded + roll(folded, shift, 1)
+    own = iota((SUB, LANE), 1) // (LANE // SUB) == iota((SUB, LANE), 0)
+    part[...] = jnp.sum(jnp.where(own, folded, 0.0), axis=0, keepdims=True)
 
     for offset in range(1, count):
         pltpu.make_async_remote_copy(
@@ -282,7 +303,8 @@
         device_id_type=MESH,
     )
     everything.wait_recv()
-    total = jnp.sum(jnp.sum(slots[...], axis=0) + part[...], axis=1, keepdims=True)
+    total = jnp.sum(slots[...], axis=0) + part[...]
+    total = jnp.sum(jnp.where(own, total, 0.0), axis=1, keepdims=True)
     moment = [total[i : i + 1, :] for i in range(2 * ITERS)]
 
     def inner(a, b):
@@ -323,6 +345,7 @@
     smem = pl.BlockSpec(memory_space=pltpu.SMEM)
     f32 = jnp.float32
     dma = pltpu.SemaphoreType.DMA
+    pairs = pl.cdiv(4 * (3 * levels + 2), 2 * SUB)
     scratch = [
         pltpu.VMEM((levels, *ext), f32),
         pltpu.VMEM((levels, *ext), f32),
@@ -330,8 +353,9 @@
         pltpu.VMEM((rows, cols), jnp.int32),
         pltpu.VMEM((rows, cols), f32),
         pltpu.VMEM((2, *ext), f32),
+        pltpu.VMEM((2, *ext), f32),
         pltpu.VMEM((rows, LANE), f32),
-        pltpu.VMEM((2, rows, LANE), f32),
+        *[pltpu.VMEM((pairs, SUB, rows), f32)] * 4,
         pltpu.VMEM((4, SUB, LANE), f32),
         pltpu.VMEM((levels, SUB, cols), f32),
         pltpu.VMEM((levels, SUB, cols), f32),
@@ -344,8 +368,8 @@
         pltpu.VMEM((2, SUB, cols), f32),
         pltpu.VMEM((2, SUB, rows), f32),
         pltpu.VMEM((4, SUB, LANE), f32),
-        pltpu.VMEM((SUB, LANE), f32),
-        pltpu.VMEM((ny * nx - 1, SUB, LANE), f32),
+        pltpu.VMEM((1, LANE), f32),
+        pltpu.VMEM((ny * nx - 1, 1, LANE), f32),
         dma((6,)),
         dma,
         dma((2 * len(AROUND),)),

time: 32.9 us -> 30 us (0.912)
  Pallas kernels: 29.1 us -> 26.3 us
    pallas_call x1, Pallas kernels: 29.1 us -> 26.3 us  [on_device(): pl.pallas_call(functools.partial(kernel, ny, nx), out_shape=(jax.ShapeDty...]
where the time goes in v2:
time: 30 us; the launch traced here: 29.9 us
  Pallas kernels  26.3 us (88%)
  local copies, waits for them, and re-layouts  2.96 us (10%)
  between operations  0.65 us (2%)
    pallas_call x1, Pallas kernels, on_device(): pl.pallas_call(functools.partial(kernel, ny, nx), out_shape=(jax.ShapeDty...  26.3 us
    unnamed x4, local copies, waits for them, and re-layouts  2.96 us

profile of v2, /device:TPU:0, one launch (start us, length us, event | category | flops | bytes accessed | tf_op | source)
XLA Modules:
  0.0 29.9 jit_solution(3485423526675414901)
XLA Ops:
  0.6 26.3 %shard_map.86 = (f32[8,128,256]{2,1,0:T(8,128)}, f32[128,256]{1,0:T(8,128)}) custom-call(f32[8,128,256]{2,1,0:T(8,128)} %tracer_ref.1, f32[8,128,256]{2,1,0:T(8,128)} %east_ref.1, f32[8,128,256]{2,1,0:T(8,128)} %north_ref.1, s32[128,256]{1,0:T(8,128)} %columns_ref.1, f32[8]{0:T(128)} %thickness_ref.1, f32[128,256]{1,0:T(8,128)} %surface_ref.1, ...), custom_call_target="tpu_custom_call" | custom-call | tf_op jit(solution)/shard_map/pallas_call | solution.py:380
  26.9 0.0 copy-start
  26.9 2.3 %copy.11 = f32[8,128,256]{2,1,0:T(8,128)} copy(f32[8,128,256]{2,1,0:T(8,128)} %get-tuple-element.4) | data formatting | bytes 2097152
  29.2 0.0 copy-done
  29.2 0.7 %copy.12 = f32[128,256]{1,0:T(8,128)} copy(f32[128,256]{1,0:T(8,128)S(1)} %copy-done) | data formatting | bytes 262144
Async XLA Ops:
  26.9 2.3 %copy-start = (f32[128,256]{1,0:T(8,128)S(1)}, f32[128,256]{1,0:T(8,128)}, u32[]{:S(2)}) copy-start(f32[128,256]{1,0:T(8,128)} %get-tuple-element.5) | copy-start | bytes 393220

commit v3 on v2

--- a/solution.py
+++ b/solution.py
@@ -160,7 +160,7 @@
                     device_id_type=MESH,
                 )
             )
-        for copy in copies:
+        for copy in reversed(copies):
             copy.start()
         return copies
 
@@ -220,7 +220,7 @@
         forcing[...] += jnp.where(open_here, thickness_ref[k] * current[0:rows, 0:cols], 0.0)
         return carry
 
-    lax.fori_loop(0, levels, level, 0)
+    lax.fori_loop(0, levels, level, 0, unroll=2)
 
     out_copy = pltpu.make_async_copy(c_ext.at[:, 0:rows, 0:cols], tracer_out, out_sem)
     out_copy.start()
@@ -335,6 +335,21 @@
     for copy in copies:
         copy.wait_send()
     out_copy.wait()
+
+
+def hand_on(tracer_ref, heights_ref, tracer_out, heights_out, tracer_held, heights_held, load, save):
+    levels = tracer_ref.shape[0]
+    stages = [(tracer_ref.at[k], tracer_held.at[k], tracer_out.at[k]) for k in range(levels)]
+    stages.append((heights_ref, heights_held, heights_out))
+    loads = [pltpu.make_async_copy(a, b, load.at[i]) for i, (a, b, _) in enumerate(stages)]
+    saves = [pltpu.make_async_copy(b, c, save.at[i]) for i, (_, b, c) in enumerate(stages)]
+    for copy in loads:
+        copy.start()
+    for copy, onward in zip(loads, saves):
+        copy.wait()
+        onward.start()
+    for onward in saves:
+        onward.wait()
 
 
 def on_device(ny, nx, tracer, east_speed, north_speed, columns, thickness, surface_flux, helm):
@@ -377,7 +392,7 @@
         dma,
         dma,
     ]
-    return pl.pallas_call(
+    results = pl.pallas_call(
         functools.partial(kernel, ny, nx),
         out_shape=(
             jax.ShapeDtypeStruct((levels, rows, cols), f32),
@@ -388,6 +403,18 @@
         scratch_shapes=scratch,
         compiler_params=pltpu.CompilerParams(collective_id=0, has_side_effects=True),
     )(tracer, east_speed, north_speed, columns, thickness, surface_flux, helm)
+    return pl.pallas_call(
+        hand_on,
+        out_shape=tuple(jax.ShapeDtypeStruct(r.shape, f32) for r in results),
+        in_specs=[hbm, hbm],
+        out_specs=(hbm, hbm),
+        scratch_shapes=[
+            pltpu.VMEM((levels, rows, cols), f32),
+            pltpu.VMEM((rows, cols), f32),
+            dma((levels + 1,)),
+            dma((levels + 1,)),
+        ],
+    )(*results)
 
 
 def solution(mesh):

time: 30 us -> 28.8 us (0.960)
  local copies, waits for them, and re-layouts: 2.96 us -> 0 us
  Pallas kernels: 26.3 us -> 28 us
    unnamed x4 -> x0, local copies, waits for them, and re-layouts: 2.96 us -> none
    pallas_call x0 -> x1, Pallas kernels: none -> 2.15 us  [on_device(): pl.pallas_call(hand_on, out_shape=tuple((jax.ShapeDtypeStruct(r.shape, f3...]
    pallas_call x1, Pallas kernels: 26.3 us -> 25.8 us  [on_device(): pl.pallas_call(functools.partial(kernel, ny, nx), out_shape=(jax.ShapeDty...]
where the time goes in v3:
time: 28.8 us; the launch traced here: 28.6 us
  Pallas kernels  28 us (97%)
  between operations  0.64 us (2%)
    pallas_call x1, Pallas kernels, on_device(): pl.pallas_call(functools.partial(kernel, ny, nx), out_shape=(jax.ShapeDty...  25.8 us
    pallas_call x1, Pallas kernels, on_device(): pl.pallas_call(hand_on, out_shape=tuple((jax.ShapeDtypeStruct(r.shape, f3...  2.15 us

profile of v3, /device:TPU:0, one launch (start us, length us, event | category | flops | bytes accessed | tf_op | source)
XLA Modules:
  0.0 28.6 jit_solution(7915946450026673684)
XLA Ops:
  0.6 25.8 %shard_map.86 = (f32[8,128,256]{2,1,0:T(8,128)}, f32[128,256]{1,0:T(8,128)}) custom-call(f32[8,128,256]{2,1,0:T(8,128)} %tracer_ref.1, f32[8,128,256]{2,1,0:T(8,128)} %east_ref.1, f32[8,128,256]{2,1,0:T(8,128)} %north_ref.1, s32[128,256]{1,0:T(8,128)} %columns_ref.1, f32[8]{0:T(128)} %thickness_ref.1, f32[128,256]{1,0:T(8,128)} %surface_ref.1, ...), custom_call_target="tpu_custom_call" | custom-call | tf_op jit(solution)/shard_map/pallas_call | solution.py:395
  26.4 2.1 %shard_map.87 = (f32[8,128,256]{2,1,0:T(8,128)}, f32[128,256]{1,0:T(8,128)}) custom-call(f32[8,128,256]{2,1,0:T(8,128)} %get-tuple-element.4.tracer_ref, f32[128,256]{1,0:T(8,128)} %get-tuple-element.5.heights_ref), custom_call_target="tpu_custom_call" | custom-call | tf_op jit(solution)/shard_map/pallas_call | solution.py:406
